TPU v7x, 128 devices: a whole 4x4x4 slice. The times are simulated.
128 devices in a mesh: section: 2 (over x_hi), dp: 16 (over z, y), mp: 4 (over x_lo, core).
Axes of the slice: x: 4 (x_hi: 2, x_lo: 2; x = x_hi * 2 + x_lo), y: 4, z: 4, core: 2. Of those that a mesh axis runs over, the one named last changes fastest.
Arguments:
- text_feats: bfloat16 [16384, 512], P('dp'), may hold values from -48 to 48
- image_feats: bfloat16 [16384, 512], P(('dp', 'mp')), may hold values from -48 to 48
- logit_scale: float32 [1], replicated, may hold values from 10 to 320
- layer_inputs: bfloat16 [2, 16384, 512], P('section', 'dp'), may hold values from -6 to 6
- w_in: bfloat16 [2, 512, 2048], P('section', None, 'mp'), may hold values from -0.25 to 0.25
- w_out: bfloat16 [2, 2048, 512], P('section', 'mp'), may hold values from -0.125 to 0.125
Outputs:
- image_grad: bfloat16 [16384, 512], P(('dp', 'mp'))
- input_grad: bfloat16 [16384, 512], P('dp', 'section')
- w_in_grad: float32 [2, 512, 2048], P('section', 'dp', 'mp')
- w_out_grad_t: float32 [2, 512, 2048], P('section', 'dp', 'mp')
All inputs are finite; a program needn't handle non-finite values.
Results may differ from a plain program's by a relative error of at most 0.017.
Values may be sent and summed in bfloat16 or wider, within the bound.
No kernel may reach another device: no remote copies, remote signals or barrier semaphores. Data moves between devices by JAX's collectives and lax.ppermute only.
A program may use at most 128 MiB of HBM per device.

v0:
```python
import jax
import jax.numpy as jnp
from jax import lax
from jax.sharding import PartitionSpec as P

MICRO = 4


def from_everyone(array, axis):
    copies = jnp.broadcast_to(array, (lax.axis_size(axis), *array.shape))
    return lax.all_to_all(copies, axis, split_axis=0, concat_axis=0, tiled=True)


def collected_together(array, axis):
    leaves = jax.tree.leaves(array)
    sequence = sorted(range(len(leaves)), key=lambda k: -leaves[k].size)
    width = (1, *leaves[sequence[0]].shape)[-1]
    lines = [
        jnp.pad(leaves[k].reshape(-1), (0, -leaves[k].size % width)).reshape(-1, width)
        for k in sequence
    ]
    both, at, found = (from_everyone(jnp.concatenate(lines), axis), 0, {})
    for k, line in zip(sequence, lines):
        slab = both[:, at : at + len(line)].reshape(len(both), -1)
        found[k] = slab[:, : leaves[k].size].reshape(-1, *leaves[k].shape)
        at += len(line)
    numbers = iter(range(len(leaves)))
    return jax.tree.map(lambda _: found[next(numbers)], array)


def combined_pairwise(pieces, combine):
    while len(jax.tree.leaves(pieces)[0]) > 1:
        pieces = jax.vmap(combine)(
            *(jax.tree.map(lambda part: part[side::2], pieces) for side in (0, 1))
        )
    return jax.tree.map(lambda part: part[0], pieces)


def joined_all(array, axis, combine):
    pieces = collected_together(array, axis)
    return combined_pairwise(pieces, combine)


def of_everyone(array, axis):
    return from_everyone(array, axis).astype(jnp.float32).sum(axis=0)


def shifted(block, axis, distance):
    devices = range(lax.axis_size(axis))
    route = [(i - distance, i) for i in devices if i - distance in devices]
    return lax.ppermute(block, axis, route)


def picked(array, axis, root):
    return lax.dynamic_index_in_dim(lax.all_gather(array, axis), root, 0, keepdims=False)


def in_one_piece(arrays, axis, dim, along):
    both = jnp.concatenate(arrays, axis=along)
    result, at, done = (lax.psum_scatter(both, axis, scatter_dimension=dim, tiled=True), 0, [])
    for a in arrays:
        done.append(lax.slice_in_dim(result, at, at + a.shape[along], axis=along))
        at += a.shape[along]
    return tuple(done)


def unit_rows(values):
    wide = values.astype(jnp.float32)
    length = jnp.sqrt(jnp.sum(wide * wide, axis=1, keepdims=True) + 1.0)
    return (wide / length, length)


def unit_backward(unit, length, grad_unit):
    return (grad_unit - unit * jnp.sum(unit * grad_unit, axis=1, keepdims=True)) / length


def quick_gelu(values):
    return values * jax.nn.sigmoid(1.702 * values)


def quick_slope(values):
    sigm = jax.nn.sigmoid(1.702 * values)
    return sigm + 1.702 * values * sigm * (1.0 - sigm)


def joined_softmax(left_pair, right_pair):
    peak_value = jnp.maximum(left_pair[0], right_pair[0])
    total = left_pair[1] * jnp.exp(left_pair[0] - peak_value) + right_pair[1] * jnp.exp(
        right_pair[0] - peak_value
    )
    return (peak_value, total)


def contract_rows(left_side, right_side):
    return lax.dot_general(
        left_side, right_side, (((0,), (0,)), ((), ())), preferred_element_type=jnp.float32
    )


def contract_cols(left_side, right_side):
    return lax.dot_general(
        left_side, right_side, (((1,), (1,)), ((), ())), preferred_element_type=jnp.float32
    )


def body(text_feats, image_feats, logit_scale, layer_inputs, w_in, w_out):
    logit_mult = logit_scale[0]
    mp_count = lax.axis_size("mp")
    segment_count = lax.axis_size("section")
    dp_index = lax.axis_index("dp")
    mp_index = lax.axis_index("mp")
    segment_index = lax.axis_index("section")
    row_count = text_feats.shape[0]
    own_rows = image_feats.shape[0]
    text_unit, text_length = unit_rows(text_feats)
    image_unit, image_length = unit_rows(image_feats)
    text_low = text_unit.astype(jnp.bfloat16)
    image_low = image_unit.astype(jnp.bfloat16)
    columns = lax.all_gather(image_low, "dp", axis=0, tiled=True)
    column_total_count = columns.shape[0]
    scores = logit_mult * contract_cols(text_low, columns)
    text_ids = dp_index * row_count + jnp.arange(row_count, dtype=jnp.int32)
    column_pos = jnp.arange(column_total_count, dtype=jnp.int32)
    image_ids = (column_pos // own_rows * mp_count + mp_index) * own_rows + column_pos % own_rows
    positive = (text_ids[:, None] == image_ids[None, :]).astype(jnp.float32)
    local_rpeak = jnp.max(scores, axis=1)
    local_cpeak = jnp.max(scores, axis=0)
    row_peak, row_total = joined_all(
        (local_rpeak, jnp.sum(jnp.exp(scores - local_rpeak[:, None]), axis=1)), "mp", joined_softmax
    )
    column_local = jnp.sum(jnp.exp(scores - local_cpeak[None, :]), axis=0)
    column_peak, column_total = joined_all((local_cpeak, column_local), "dp", joined_softmax)
    row_prob = jnp.exp(scores - row_peak[:, None]) / row_total[:, None]
    column_prob = jnp.exp(scores - column_peak[None, :]) / column_total[None, :]
    score_grad = (0.5 * (row_prob + column_prob) - positive).astype(jnp.bfloat16)
    text_share = logit_mult * jnp.dot(score_grad, columns, preferred_element_type=jnp.float32)
    text_unit_grad = of_everyone(text_share.astype(jnp.bfloat16), "mp").astype(jnp.float32)
    top_grad = unit_backward(text_unit, text_length, text_unit_grad).astype(jnp.bfloat16)
    image_unit_grad = lax.psum_scatter(
        (logit_mult * contract_rows(score_grad, text_low)).astype(jnp.bfloat16),
        "dp",
        scatter_dimension=0,
        tiled=True,
    ).astype(jnp.float32)
    image_grad = unit_backward(image_unit, image_length, image_unit_grad).astype(jnp.bfloat16)
    segment_inputs = layer_inputs[0]
    w_first = w_in[0]
    w_second = w_out[0]
    step_rows = row_count // MICRO
    last_segment = segment_count - 1
    time_steps = MICRO + segment_count - 1
    is_last = segment_index == last_segment
    is_first = segment_index == 0
    incoming = jnp.zeros((step_rows, segment_inputs.shape[1]), jnp.bfloat16)
    grad_first = jnp.zeros(w_first.shape, jnp.float32)
    grad_second = jnp.zeros(w_first.shape, jnp.float32)
    finished = jnp.zeros((row_count, segment_inputs.shape[1]), jnp.bfloat16)
    for time_step in range(time_steps):
        micro_slot = time_step - last_segment + segment_index
        active = jnp.logical_and(micro_slot >= 0, micro_slot < MICRO)
        row_start = jnp.clip(micro_slot, 0, MICRO - 1) * step_rows
        top_start = min(time_step, MICRO - 1) * step_rows
        top_piece = top_grad[top_start : top_start + step_rows]
        grad_now = jnp.where(is_last, top_piece, incoming)
        inputs_now = lax.dynamic_slice_in_dim(segment_inputs, row_start, step_rows, 0)
        pre_act = jnp.dot(inputs_now, w_first, preferred_element_type=jnp.float32)
        activation = quick_gelu(pre_act).astype(jnp.bfloat16)
        back_grad = contract_cols(grad_now, w_second)
        pre_grad = (back_grad * quick_slope(pre_act)).astype(jnp.bfloat16)
        unit_share = contract_cols(pre_grad, w_first)
        summed = of_everyone(unit_share.astype(jnp.bfloat16), "mp").astype(jnp.float32)
        grad_prev = (grad_now.astype(jnp.float32) + summed).astype(jnp.bfloat16)
        weight = active.astype(jnp.float32)
        grad_first = grad_first + weight * contract_rows(inputs_now, pre_grad)
        grad_second = grad_second + weight * contract_rows(grad_now, activation)
        updated = lax.dynamic_update_slice_in_dim(finished, grad_prev, row_start, 0)
        finished = jnp.where(jnp.logical_and(active, is_first), updated, finished)
        if time_step + 1 < time_steps:
            incoming = shifted(grad_prev, "section", -1)
    whole_grad = picked(finished, "section", 0)
    feature_width = whole_grad.shape[1] // segment_count
    feature_start = segment_index * feature_width
    input_grad = lax.dynamic_slice_in_dim(whole_grad, feature_start, feature_width, 1)
    first_sum, second_sum = tuple(
        (
            part.astype(jnp.float32)
            for part in in_one_piece(
                (grad_first.astype(jnp.bfloat16), grad_second.astype(jnp.bfloat16)), "dp", 0, 1
            )
        )
    )
    return (image_grad, input_grad, first_sum[None], second_sum[None])


def solution(mesh):
    placed = (
        P("dp", None),
        P(("dp", "mp"), None),
        P(),
        P("section", "dp", None),
        P("section", None, "mp"),
        P("section", "mp", None),
    )
    return jax.shard_map(
        body,
        mesh=mesh,
        in_specs=placed,
        out_specs=(
            P(("dp", "mp"), None),
            P("dp", "section"),
            P("section", "dp", "mp"),
            P("section", "dp", "mp"),
        ),
        check_vma=False,
    )
```

profile of v0, /device:TPU:1, one launch (start us, length us, event | category | flops | bytes accessed | tf_op | source)
XLA Modules:
  0.0 463.0 jit_solution(3558980149796986611)
XLA Ops:
  12.4 52.9 %all-gather.3.cloned.1.call-done = bf16[4096,512]{1,0:T(8,128)(2,1)} async-done(((bf16[256,512]{1,0:T(8,128)(2,1)}), bf16[4096,512]{1,0:T(8,128)(2,1)}) %all-gather.3.cloned.1.call-update) | async-done | bytes 4194320 | tf_op jit(solution)/shard_map/all_gather | solution.py:119
  65.3 6.8 %multiply_reduce_fusion.1 = (f32[1024]{0:T(1024)S(1)}, f32[1024,4096]{1,0:T(8,128)S(1)}) fusion(f32[]{:T(128)} %bitcast.111, bf16[4096,512]{1,0:T(8,128)(2,1)} %all-gather.3.cloned.1.call-done, f32[1024]{0:T(1024)S(1)} %add_sqrt_fusion, bf16[1024,512]{1,0:T(8,128)(2,1)} %param.6), kind=kOutput, calls=%fused_computation.4 | convolution fusion | flops 4304927744 | bytes 22028292 | tf_op jit(solution)/shard_map/dot_general | solution.py:101
  72.1 4.3 exponential_reduce_fusion.1
  78.5 4.1 all-to-all-start
  82.6 8.5 %exponential_reduce_fusion = f32[4096]{0:T(1024)S(1)} fusion(f32[1024,4096]{1,0:T(8,128)} %copy-done.1, f32[4096]{0:T(1024)S(1)} %get-tuple-element.17, f32[]{:T(128)} %bitcast.115), kind=kLoop, calls=%fused_computation.1 | loop fusion | flops 12578816 | bytes 16809988 | tf_op jit(solution)/shard_map/reduce_sum | solution.py:131
  92.1 5.0 %all-to-all-start.1 = ((f32[16,2,4096]{2,1,0:T(2,128)}), f32[16,2,4096]{2,1,0:T(2,128)S(1)}, u32[]{:S(2)}, u32[]{:S(2)}) async-start(f32[16,2,4096]{2,1,0:T(2,128)} %broadcast_in_dim.51), calls=%async_computation.1 | async-start | bytes 1048576 | tf_op jit(solution)/shard_map/all_to_all | solution.py:11
  97.4 10.8 %all-to-all-done.1 = f32[16,2,4096]{2,1,0:T(2,128)S(1)} async-done(((f32[16,2,4096]{2,1,0:T(2,128)}), f32[16,2,4096]{2,1,0:T(2,128)S(1)}, u32[]{:S(2)}, u32[]{:S(2)}) %all-to-all-start.1) | async-done | bytes 524320 | tf_op jit(solution)/shard_map/all_to_all | solution.py:11
  110.7 11.4 %subtract_convert_fusion = bf16[1024,4096]{1,0:T(8,128)(2,1)S(1)} fusion(f32[1024,4096]{1,0:T(8,128)} %copy-done.1, s32[4096]{0:T(1024)S(1)} %fusion.87, f32[4096]{0:T(1024)S(1)} %bitcast.117, f32[4096]{0:T(1024)S(1)} %bitcast.118, f32[1024]{0:T(1024)S(1)} %bitcast.120, f32[1024]{0:T(1024)S(1)} %bitcast.121, f32[]{:T(128)} %bitcast.114, s32[1024]{0:T(1024)S(1)} %iota_add_fusion), kind=kLoop, calls=%fused_computation | loop fusion | flops 46137344 | bytes 25227268 | tf_op jit(solution)/shard_map/convert_element_type | solution.py:135
  122.1 3.3 copy-done.4
  125.4 4.5 multiply_convert_fusion.1
  132.1 6.5 %all-to-all-start.2 = ((bf16[4,1024,512]{2,1,0:T(8,128)(2,1)}), bf16[4,1024,512]{2,1,0:T(8,128)(2,1)}, u32[]{:S(2)}, u32[]{:S(2)}) async-start(bf16[4,1024,512]{2,1,0:T(8,128)(2,1)} %broadcast_in_dim.53), calls=%async_computation.3 | async-start | bytes 8388608 | tf_op jit(solution)/shard_map/all_to_all | solution.py:11
  139.0 47.0 %all-to-all-done.2 = bf16[4,1024,512]{2,1,0:T(8,128)(2,1)} async-done(((bf16[4,1024,512]{2,1,0:T(8,128)(2,1)}), bf16[4,1024,512]{2,1,0:T(8,128)(2,1)}, u32[]{:S(2)}, u32[]{:S(2)}) %all-to-all-start.2) | async-done | bytes 4194336 | tf_op jit(solution)/shard_map/all_to_all | solution.py:11
  185.9 3.2 convert_reduce_fusion
  193.7 5.2 %all-to-all-start.3 = ((bf16[4,256,512]{2,1,0:T(8,128)(2,1)}), bf16[4,256,512]{2,1,0:T(8,128)(2,1)}, u32[]{:S(2)}, u32[]{:S(2)}) async-start(bf16[4,256,512]{2,1,0:T(8,128)(2,1)} %broadcast_in_dim.55), calls=%async_computation.4 | async-start | bytes 2097152 | tf_op jit(solution)/shard_map/all_to_all | solution.py:11
  199.2 13.3 %all-to-all-done.3 = bf16[4,256,512]{2,1,0:T(8,128)(2,1)} async-done(((bf16[4,256,512]{2,1,0:T(8,128)(2,1)}), bf16[4,256,512]{2,1,0:T(8,128)(2,1)}, u32[]{:S(2)}, u32[]{:S(2)}) %all-to-all-start.3) | async-done | bytes 1048608 | tf_op jit(solution)/shard_map/all_to_all | solution.py:11
  218.2 9.9 %multiply_convert_fusion = bf16[4096,512]{1,0:T(8,128)(2,1)} fusion(bf16[1024,4096]{1,0:T(8,128)(2,1)} %copy-done.4, f32[]{:T(128)} %bitcast.110, bf16[1024,512]{1,0:T(8,128)(2,1)S(1)} %copy-done.3, f32[1024]{0:T(1024)S(1)} %add_sqrt_fusion), kind=kOutput, calls=%fused_computation.6 | convolution fusion | flops 4300734464 | bytes 13635588 | tf_op jit(solution)/shard_map/dot_general | solution.py:95
  232.9 5.2 %all-to-all-start.4 = ((bf16[4,256,512]{2,1,0:T(8,128)(2,1)}), bf16[4,256,512]{2,1,0:T(8,128)(2,1)}, u32[]{:S(2)}, u32[]{:S(2)}) async-start(bf16[4,256,512]{2,1,0:T(8,128)(2,1)} %broadcast_in_dim.56), calls=%async_computation.5 | async-start | bytes 2097152 | tf_op jit(solution)/shard_map/all_to_all | solution.py:11
  238.1 13.6 %all-to-all-done.4 = bf16[4,256,512]{2,1,0:T(8,128)(2,1)} async-done(((bf16[4,256,512]{2,1,0:T(8,128)(2,1)}), bf16[4,256,512]{2,1,0:T(8,128)(2,1)}, u32[]{:S(2)}, u32[]{:S(2)}) %all-to-all-start.4) | async-done | bytes 1048608 | tf_op jit(solution)/shard_map/all_to_all | solution.py:11
  256.6 9.9 %collective-permute-done.1 = bf16[256,512]{1,0:T(8,128)(2,1)} collective-permute-done((bf16[256,512]{1,0:T(8,128)(2,1)}, bf16[256,512]{1,0:T(8,128)(2,1)}, u32[]{:S(2)}, u32[]{:S(2)}) %collective-permute-start.1) | collective-permute-done | bytes 262176 | tf_op jit(solution)/shard_map/ppermute | solution.py:51
  271.1 5.7 %all-to-all-start.5 = ((bf16[4,256,512]{2,1,0:T(8,128)(2,1)}), bf16[4,256,512]{2,1,0:T(8,128)(2,1)}, u32[]{:S(2)}, u32[]{:S(2)}) async-start(bf16[4,256,512]{2,1,0:T(8,128)(2,1)} %broadcast_in_dim.57), calls=%async_computation.6 | async-start | bytes 2097152 | tf_op jit(solution)/shard_map/all_to_all | solution.py:11
  281.3 2.4 convolution_multiply_fusion.4
  283.7 6.6 %all-to-all-done.5 = bf16[4,256,512]{2,1,0:T(8,128)(2,1)} async-done(((bf16[4,256,512]{2,1,0:T(8,128)(2,1)}), bf16[4,256,512]{2,1,0:T(8,128)(2,1)}, u32[]{:S(2)}, u32[]{:S(2)}) %all-to-all-start.5) | async-done | bytes 1048608 | tf_op jit(solution)/shard_map/all_to_all | solution.py:11
  294.9 2.8 fusion.2
  297.7 6.2 %collective-permute-done.2 = bf16[256,512]{1,0:T(8,128)(2,1)S(1)} collective-permute-done((bf16[256,512]{1,0:T(8,128)(2,1)S(1)}, bf16[256,512]{1,0:T(8,128)(2,1)S(1)}, u32[]{:S(2)}, u32[]{:S(2)}) %collective-permute-start.2) | collective-permute-done | bytes 262176 | tf_op jit(solution)/shard_map/ppermute | solution.py:51
  308.4 6.0 %all-to-all-start.6 = ((bf16[4,256,512]{2,1,0:T(8,128)(2,1)}), bf16[4,256,512]{2,1,0:T(8,128)(2,1)}, u32[]{:S(2)}, u32[]{:S(2)}) async-start(bf16[4,256,512]{2,1,0:T(8,128)(2,1)} %broadcast_in_dim.58), calls=%async_computation.7 | async-start | bytes 2097152 | tf_op jit(solution)/shard_map/all_to_all | solution.py:11
  317.3 2.3 fusion.4
  319.6 8.3 %all-to-all-done.6 = bf16[4,256,512]{2,1,0:T(8,128)(2,1)} async-done(((bf16[4,256,512]{2,1,0:T(8,128)(2,1)}), bf16[4,256,512]{2,1,0:T(8,128)(2,1)}, u32[]{:S(2)}, u32[]{:S(2)}) %all-to-all-start.6) | async-done | bytes 1048608 | tf_op jit(solution)/shard_map/all_to_all | solution.py:11
  334.1 7.5 %collective-permute-done.3 = bf16[256,512]{1,0:T(8,128)(2,1)S(1)} collective-permute-done((bf16[256,512]{1,0:T(8,128)(2,1)S(1)}, bf16[256,512]{1,0:T(8,128)(2,1)S(1)}, u32[]{:S(2)}, u32[]{:S(2)}) %collective-permute-start.3) | collective-permute-done | bytes 262176 | tf_op jit(solution)/shard_map/ppermute | solution.py:51
  348.5 5.3 %all-to-all-start.7 = ((bf16[4,256,512]{2,1,0:T(8,128)(2,1)}), bf16[4,256,512]{2,1,0:T(8,128)(2,1)S(1)}, u32[]{:S(2)}, u32[]{:S(2)}) async-start(bf16[4,256,512]{2,1,0:T(8,128)(2,1)} %broadcast_in_dim.59), calls=%async_computation.8 | async-start | bytes 2097152 | tf_op jit(solution)/shard_map/all_to_all | solution.py:11
  356.0 11.3 %all-to-all-done.7 = bf16[4,256,512]{2,1,0:T(8,128)(2,1)S(1)} async-done(((bf16[4,256,512]{2,1,0:T(8,128)(2,1)}), bf16[4,256,512]{2,1,0:T(8,128)(2,1)S(1)}, u32[]{:S(2)}, u32[]{:S(2)}) %all-to-all-start.7) | async-done | bytes 1048608 | tf_op jit(solution)/shard_map/all_to_all | solution.py:11
  372.4 42.6 %reduce-scatter.7.cloned.1.call-done = bf16[32,1024]{1,0:T(8,128)(2,1)} async-done(((bf16[512,1024]{1,0:T(8,128)(2,1)}), bf16[32,1024]{1,0:T(8,128)(2,1)}) %reduce-scatter.7.cloned.1.call-update) | async-done | bytes 65552
  417.5 36.8 %all-gather.5.cloned.1.call-done = bf16[2,1024,512]{2,1,0:T(8,128)(2,1)} async-done(((bf16[1,1024,512]{2,1,0:T(8,128)(2,1)}), bf16[2,1024,512]{2,1,0:T(8,128)(2,1)}) %all-gather.5.cloned.1.call-update) | async-done | bytes 2097168 | tf_op jit(solution)/shard_map/all_gather | solution.py:55
  (158 shorter events, 78.7 us)
Async XLA Ops:
  7.2 131.5 %copy-start = (bf16[1,1024,512]{2,1,0:T(8,128)(2,1)S(1)}, bf16[1,1024,512]{2,1,0:T(8,128)(2,1)}, u32[]{:S(2)}) copy-start(bf16[1,1024,512]{2,1,0:T(8,128)(2,1)} %param.9) | copy-start | bytes 3145732
  7.2 58.1 %all-gather.3.cloned.1.call-start = ((), (), s32[]{:S(2)}) async-start(), calls=%async_computation.10 | async-start | bytes 4456448 | tf_op jit(solution)/shard_map/all_gather | solution.py:119
  72.1 5.7 %copy-start.1 = (f32[1024,4096]{1,0:T(8,128)}, f32[1024,4096]{1,0:T(8,128)S(1)}, u32[]{:S(2)}) copy-start(f32[1024,4096]{1,0:T(8,128)S(1)} %get-tuple-element.45) | copy-start | bytes 50331652
  78.5 12.6 %all-to-all-start = ((f32[4,2,1024]{2,1,0:T(2,128)}), f32[4,2,1024]{2,1,0:T(2,128)S(1)}, u32[]{:S(2)}, u32[]{:S(2)}) async-start(f32[4,2,1024]{2,1,0:T(2,128)} %broadcast_in_dim.50), calls=%async_computation | async-start | bytes 65536 | tf_op jit(solution)/shard_map/all_to_all | solution.py:11
  92.1 16.0 %all-to-all-start.1 = ((f32[16,2,4096]{2,1,0:T(2,128)}), f32[16,2,4096]{2,1,0:T(2,128)S(1)}, u32[]{:S(2)}, u32[]{:S(2)}) async-start(f32[16,2,4096]{2,1,0:T(2,128)} %broadcast_in_dim.51), calls=%async_computation.1 | async-start | bytes 1048576 | tf_op jit(solution)/shard_map/all_to_all | solution.py:11
  110.7 14.7 %copy-start.22 = (bf16[4096,512]{1,0:T(8,128)(2,1)S(1)}, bf16[4096,512]{1,0:T(8,128)(2,1)}, u32[]{:S(2)}) copy-start(bf16[4096,512]{1,0:T(8,128)(2,1)} %all-gather.3.cloned.1.call-done) | copy-start | bytes 12582916
  122.1 3.3 copy-start.4
  129.9 8.8 %copy-start.2 = (bf16[1,512,512]{2,1,0:T(8,128)(2,1)S(1)}, bf16[1,512,512]{2,1,0:T(8,128)(2,1)}, u32[]{:S(2)}) copy-start(bf16[1,512,512]{2,1,0:T(8,128)(2,1)} %param.10) | copy-start | bytes 1572868
  132.1 57.0 %copy-start.3 = (bf16[1024,512]{1,0:T(8,128)(2,1)S(1)}, bf16[1024,512]{1,0:T(8,128)(2,1)}, u32[]{:S(2)}) copy-start(bf16[1024,512]{1,0:T(8,128)(2,1)} %param.6) | copy-start | bytes 3145732
  132.1 53.8 %all-to-all-start.2 = ((bf16[4,1024,512]{2,1,0:T(8,128)(2,1)}), bf16[4,1024,512]{2,1,0:T(8,128)(2,1)}, u32[]{:S(2)}, u32[]{:S(2)}) async-start(bf16[4,1024,512]{2,1,0:T(8,128)(2,1)} %broadcast_in_dim.53), calls=%async_computation.3 | async-start | bytes 8388608 | tf_op jit(solution)/shard_map/all_to_all | solution.py:11
  139.0 52.6 %copy-start.19 = (f32[256,512]{1,0:T(8,128)}, f32[256,512]{1,0:T(8,128)S(1)}, u32[]{:S(2)}) copy-start(f32[256,512]{1,0:T(8,128)S(1)} %fusion.33) | copy-start | bytes 1572868
  185.9 5.2 %copy-start.23 = (bf16[1,512,512]{2,1,0:T(8,128)(2,1)S(1)}, bf16[1,512,512]{2,1,0:T(8,128)(2,1)}, u32[]{:S(2)}) copy-start(bf16[1,512,512]{2,1,0:T(8,128)(2,1)} %param.11) | copy-start | bytes 1572868
  193.7 18.8 %all-to-all-start.3 = ((bf16[4,256,512]{2,1,0:T(8,128)(2,1)}), bf16[4,256,512]{2,1,0:T(8,128)(2,1)}, u32[]{:S(2)}, u32[]{:S(2)}) async-start(bf16[4,256,512]{2,1,0:T(8,128)(2,1)} %broadcast_in_dim.55), calls=%async_computation.4 | async-start | bytes 2097152 | tf_op jit(solution)/shard_map/all_to_all | solution.py:11
  198.9 170.4 %reduce-scatter.5.cloned.1.call-start = ((), (), s32[]{:S(2)}) async-start(), calls=%async_computation.11 | async-start | bytes 4456448 | tf_op jit(solution)/shard_map/reduce_scatter | solution.py:139
  199.2 30.1 %copy-start.20 = (f32[256,512]{1,0:T(8,128)}, f32[256,512]{1,0:T(8,128)S(1)}, u32[]{:S(2)}) copy-start(f32[256,512]{1,0:T(8,128)S(1)} %fusion.30) | copy-start | bytes 1572868
  216.7 11.4 %collective-permute-start = (bf16[256,512]{1,0:T(8,128)(2,1)S(1)}, bf16[256,512]{1,0:T(8,128)(2,1)}, u32[]{:S(2)}, u32[]{:S(2)}) collective-permute-start(bf16[256,512]{1,0:T(8,128)(2,1)S(1)} %get-tuple-element.25), channel_id=1, source_target_pairs={{64,0},{65,1},{66,2},{67,3},{68,4},{69,5},{70,6},{71,7},{72,8},{73... | collective-permute-start | bytes 786440 | tf_op jit(solution)/shard_map/ppermute | solution.py:51
  228.1 38.4 %copy-start.6 = (bf16[1024,512]{1,0:T(8,128)(2,1)S(1)}, bf16[1024,512]{1,0:T(8,128)(2,1)}, u32[]{:S(2)}) copy-start(bf16[1024,512]{1,0:T(8,128)(2,1)} %copy-done.5) | copy-start | bytes 3145732
  229.3 27.3 %copy-start.14 = (bf16[256,512]{1,0:T(8,128)(2,1)}, bf16[256,512]{1,0:T(8,128)(2,1)S(1)}, u32[]{:S(2)}) copy-start(bf16[256,512]{1,0:T(8,128)(2,1)S(1)} %slice_select_fusion.1) | copy-start | bytes 786436
  232.9 18.7 %all-to-all-start.4 = ((bf16[4,256,512]{2,1,0:T(8,128)(2,1)}), bf16[4,256,512]{2,1,0:T(8,128)(2,1)}, u32[]{:S(2)}, u32[]{:S(2)}) async-start(bf16[4,256,512]{2,1,0:T(8,128)(2,1)} %broadcast_in_dim.56), calls=%async_computation.5 | async-start | bytes 2097152 | tf_op jit(solution)/shard_map/all_to_all | solution.py:11
  255.0 11.5 %collective-permute-start.1 = (bf16[256,512]{1,0:T(8,128)(2,1)}, bf16[256,512]{1,0:T(8,128)(2,1)}, u32[]{:S(2)}, u32[]{:S(2)}) collective-permute-start(bf16[256,512]{1,0:T(8,128)(2,1)} %get-tuple-element.23), channel_id=1, source_target_pairs={{64,0},{65,1},{66,2},{67,3},{68,4},{69,5},{70,6},{71,7},{72,8},{73... | collective-permute-start | bytes 786440 | tf_op jit(solution)/shard_map/ppermute | solution.py:51
  271.1 19.3 %all-to-all-start.5 = ((bf16[4,256,512]{2,1,0:T(8,128)(2,1)}), bf16[4,256,512]{2,1,0:T(8,128)(2,1)}, u32[]{:S(2)}, u32[]{:S(2)}) async-start(bf16[4,256,512]{2,1,0:T(8,128)(2,1)} %broadcast_in_dim.57), calls=%async_computation.6 | async-start | bytes 2097152 | tf_op jit(solution)/shard_map/all_to_all | solution.py:11
  293.6 10.3 %collective-permute-start.2 = (bf16[256,512]{1,0:T(8,128)(2,1)S(1)}, bf16[256,512]{1,0:T(8,128)(2,1)S(1)}, u32[]{:S(2)}, u32[]{:S(2)}) collective-permute-start(bf16[256,512]{1,0:T(8,128)(2,1)S(1)} %get-tuple-element.21), channel_id=1, source_target_pairs={{64,0},{65,1},{66,2},{67,3},{68,4},{69,5},{70,6},{71,7},{72,8},{73... | collective-permute-start | bytes 786440 | tf_op jit(solution)/shard_map/ppermute | solution.py:51
  308.4 19.6 %all-to-all-start.6 = ((bf16[4,256,512]{2,1,0:T(8,128)(2,1)}), bf16[4,256,512]{2,1,0:T(8,128)(2,1)}, u32[]{:S(2)}, u32[]{:S(2)}) async-start(bf16[4,256,512]{2,1,0:T(8,128)(2,1)} %broadcast_in_dim.58), calls=%async_computation.7 | async-start | bytes 2097152 | tf_op jit(solution)/shard_map/all_to_all | solution.py:11
  314.3 100.6 %reduce-scatter.7.cloned.1.call-start = ((), (), s32[]{:S(2)}) async-start(), calls=%async_computation.13 | async-start | bytes 1114112
  327.9 15.4 %copy-start.21 = (f32[256,512]{1,0:T(8,128)S(1)}, f32[256,512]{1,0:T(8,128)}, u32[]{:S(2)}) copy-start(f32[256,512]{1,0:T(8,128)} %fusion.21) | copy-start | bytes 1572868
  327.9 15.8 %copy-start.7 = (f32[512,512]{0,1:T(8,128)S(1)}, f32[512,512]{0,1:T(8,128)}, u32[]{:S(2)}) copy-start(f32[512,512]{0,1:T(8,128)} %fusion.4) | copy-start | bytes 3145732
  327.9 16.2 %copy-start.9 = (f32[512,512]{0,1:T(8,128)S(1)}, f32[512,512]{0,1:T(8,128)}, u32[]{:S(2)}) copy-start(f32[512,512]{0,1:T(8,128)} %fusion.2) | copy-start | bytes 3145732
  331.3 10.3 %collective-permute-start.3 = (bf16[256,512]{1,0:T(8,128)(2,1)S(1)}, bf16[256,512]{1,0:T(8,128)(2,1)S(1)}, u32[]{:S(2)}, u32[]{:S(2)}) collective-permute-start(bf16[256,512]{1,0:T(8,128)(2,1)S(1)} %get-tuple-element.19), channel_id=1, source_target_pairs={{64,0},{65,1},{66,2},{67,3},{68,4},{69,5},{70,6},{71,7},{72,8},{73... | collective-permute-start | bytes 786440 | tf_op jit(solution)/shard_map/ppermute | solution.py:51
  344.6 22.9 %copy-start.16 = (bf16[256,512]{1,0:T(8,128)(2,1)S(1)}, bf16[256,512]{1,0:T(8,128)(2,1)}, u32[]{:S(2)}) copy-start(bf16[256,512]{1,0:T(8,128)(2,1)} %copy-done.15) | copy-start | bytes 786436
  344.6 24.7 %copy-start.8 = (bf16[256,512]{1,0:T(8,128)(2,1)S(1)}, bf16[256,512]{1,0:T(8,128)(2,1)}, u32[]{:S(2)}) copy-start(bf16[256,512]{1,0:T(8,128)(2,1)} %param.7) | copy-start | bytes 786436
  348.5 18.9 %all-to-all-start.7 = ((bf16[4,256,512]{2,1,0:T(8,128)(2,1)}), bf16[4,256,512]{2,1,0:T(8,128)(2,1)S(1)}, u32[]{:S(2)}, u32[]{:S(2)}) async-start(bf16[4,256,512]{2,1,0:T(8,128)(2,1)} %broadcast_in_dim.59), calls=%async_computation.8 | async-start | bytes 2097152 | tf_op jit(solution)/shard_map/all_to_all | solution.py:11
  353.8 100.5 %all-gather.5.cloned.1.call-start = ((), (), s32[]{:S(2)}) async-start(), calls=%async_computation.12 | async-start | bytes 3145728 | tf_op jit(solution)/shard_map/all_gather | solution.py:55
  (8 other events, 7.8 us)
Sparse Core Ops, SparseCore 0:
  10.7 54.5 all-gather.2
  228.2 76.3 reduce-scatter.4
  346.2 68.7 reduce-scatter.6
  416.4 37.8 all-gather.4
where the time goes:
time: 465 us; the launch traced here: 463 us
  waiting for transfers between devices  267 us (57%)
  other arithmetic  53.6 us (12%)
  matrix products  49 us (11%)
  starting transfers between devices  48.3 us (10%)
  local copies, waits for them, and re-layouts  30 us (6%)
  between operations  15.2 us (3%)
    all_to_all x8, waiting for transfers between devices, from_everyone(): return lax.all_to_all(copies, axis, split_axis=0, concat_axis=0, tiled=True)  111 us
    all_gather x1, waiting for transfers between devices, body(): columns = lax.all_gather(image_low, 'dp', axis=0, tiled=True)  52.9 us
    all_to_all x8, starting transfers between devices, from_everyone(): return lax.all_to_all(copies, axis, split_axis=0, concat_axis=0, tiled=True)  42.9 us
    unnamed x5, waiting for transfers between devices  42.6 us
    all_gather x1, waiting for transfers between devices, picked(): lax.all_gather(array, axis)  36.8 us
    dot_general x11, matrix products, contract_rows(): lax.dot_general(left_side, right_side, (((0,), (0,)), ((), ())), preferre...  25.3 us
    ppermute x4, waiting for transfers between devices, shifted(): return lax.ppermute(block, axis, route)  23.6 us
    dot_general x11, matrix products, contract_cols(): lax.dot_general(left_side, right_side, (((1,), (1,)), ((), ())), preferre...  16.1 us
  transfers between devices with their start and end apart: 16, of which 13 were waited for; matrix products, arithmetic and copies ran while one was open for 16% of the time, Pallas kernels for 0%

commit v1 on v0

--- a/solution.py
+++ b/solution.py
@@ -116,7 +116,8 @@
     image_unit, image_length = unit_rows(image_feats)
     text_low = text_unit.astype(jnp.bfloat16)
     image_low = image_unit.astype(jnp.bfloat16)
-    columns = lax.all_gather(image_low, "dp", axis=0, tiled=True)
+    copies_2 = jnp.concatenate([image_low] * lax.axis_size("dp"), axis=0)
+    columns = lax.all_to_all(copies_2, "dp", 0, 0, tiled=True)
     column_total_count = columns.shape[0]
     scores = logit_mult * contract_cols(text_low, columns)
     text_ids = dp_index * row_count + jnp.arange(row_count, dtype=jnp.int32)

time: 465 us -> 456 us (0.981)
  waiting for transfers between devices: 267 us -> 240 us
  starting transfers between devices: 48.3 us -> 57.5 us
    all_to_all x0 -> x1, waiting for transfers between devices: none -> 61.5 us  [body(): columns = lax.all_to_all(copies_2, 'dp', 0, 0, tiled=True)]
    all_gather x1 -> x0, waiting for transfers between devices: 52.9 us -> none  [body(): columns = lax.all_gather(image_low, 'dp', axis=0, tiled=True)]
    all_gather x1, waiting for transfers between devices: 36.8 us -> 0.01 us  [picked(): lax.all_gather(array, axis)]
    unnamed x0 -> x15, other arithmetic: none -> 9.36 us
    all_to_all x0 -> x1, starting transfers between devices: none -> 8.77 us  [body(): columns = lax.all_to_all(copies_2, 'dp', 0, 0, tiled=True)]
    unnamed x54 -> x62, local copies, waits for them, and re-layouts: 14.5 us -> 17.9 us
    unnamed x5 -> x4, waiting for transfers between devices: 42.6 us -> 43.3 us
  transfers between devices with their start and end apart: 16 -> 16, of which waited for: 13 -> 12; matrix products, arithmetic and copies ran while one was open for 16% -> 15% of each run, Pallas kernels for 0% -> 0%
where the time goes in v1:
time: 456 us; the launch traced here: 453 us
  waiting for transfers between devices  240 us (53%)
  other arithmetic  58.1 us (13%)
  starting transfers between devices  57.5 us (13%)
  matrix products  47.3 us (10%)
  local copies, waits for them, and re-layouts  33.5 us (7%)
  between operations  17 us (4%)
    all_to_all x8, waiting for transfers between devices, from_everyone(): return lax.all_to_all(copies, axis, split_axis=0, concat_axis=0, tiled=True)  112 us
    all_to_all x1, waiting for transfers between devices, body(): columns = lax.all_to_all(copies_2, 'dp', 0, 0, tiled=True)  61.5 us
    all_to_all x8, starting transfers between devices, from_everyone(): return lax.all_to_all(copies, axis, split_axis=0, concat_axis=0, tiled=True)  43.3 us
    unnamed x4, waiting for transfers between devices  43.3 us
    dot_general x11, matrix products, contract_rows(): lax.dot_general(left_side, right_side, (((0,), (0,)), ((), ())), preferre...  24.3 us
    ppermute x4, waiting for transfers between devices, shifted(): return lax.ppermute(block, axis, route)  23.1 us
    unnamed x62, local copies, waits for them, and re-layouts  17.9 us
    dot_general x11, matrix products, contract_cols(): lax.dot_general(left_side, right_side, (((1,), (1,)), ((), ())), preferre...  12.4 us
  transfers between devices with their start and end apart: 16, of which 12 were waited for; matrix products, arithmetic and copies ran while one was open for 15% of the time, Pallas kernels for 0%

profile of v1, /device:TPU:1, one launch (start us, length us, event | category | flops | bytes accessed | tf_op | source)
XLA Modules:
  0.0 453.3 jit_solution(14413090849664847572)
XLA Ops:
  20.8 8.8 %all-to-all-start = ((bf16[16,256,512]{2,1,0:T(8,128)(2,1)}), bf16[16,256,512]{2,1,0:T(8,128)(2,1)}, u32[]{:S(2)}, u32[]{:S(2)}) async-start(bf16[16,256,512]{2,1,0:T(8,128)(2,1)} %bitcast.118), calls=%async_computation | async-start | bytes 8388608 | tf_op jit(solution)/shard_map/all_to_all | solution.py:120
  30.5 61.5 %all-to-all-done = bf16[16,256,512]{2,1,0:T(8,128)(2,1)} async-done(((bf16[16,256,512]{2,1,0:T(8,128)(2,1)}), bf16[16,256,512]{2,1,0:T(8,128)(2,1)}, u32[]{:S(2)}, u32[]{:S(2)}) %all-to-all-start) | async-done | bytes 4194336 | tf_op jit(solution)/shard_map/all_to_all | solution.py:120
  92.0 6.6 %multiply_reduce_fusion.1 = (f32[1024]{0:T(1024)S(1)}, f32[1024,4096]{1,0:T(8,128)S(1)}) fusion(f32[]{:T(128)} %bitcast.113, bf16[4096,512]{1,0:T(8,128)(2,1)} %bitcast.2, f32[1024]{0:T(1024)S(1)} %add_sqrt_fusion, bf16[1024,512]{1,0:T(8,128)(2,1)S(1)} %copy-done.4), kind=kOutput, calls=%fused_computation.4 | convolution fusion | flops 4304927744 | bytes 22028292 | tf_op jit(solution)/shard_map/dot_general | solution.py:101
  98.6 4.3 exponential_reduce_fusion.1
  105.0 5.0 %all-to-all-start.1 = ((f32[4,2,1024]{2,1,0:T(2,128)}), f32[4,2,1024]{2,1,0:T(2,128)S(1)}, u32[]{:S(2)}, u32[]{:S(2)}) async-start(f32[4,2,1024]{2,1,0:T(2,128)} %broadcast_in_dim.50), calls=%async_computation.1 | async-start | bytes 65536 | tf_op jit(solution)/shard_map/all_to_all | solution.py:11
  110.0 8.5 %exponential_reduce_fusion = f32[4096]{0:T(1024)S(1)} fusion(f32[1024,4096]{1,0:T(8,128)} %copy-done.1, f32[4096]{0:T(1024)S(1)} %get-tuple-element.17, f32[]{:T(128)} %bitcast.117), kind=kLoop, calls=%fused_computation.1 | loop fusion | flops 12578816 | bytes 16809988 | tf_op jit(solution)/shard_map/reduce_sum | solution.py:132
  119.5 4.4 all-to-all-start.2
  124.2 10.8 %all-to-all-done.2 = f32[16,2,4096]{2,1,0:T(2,128)S(1)} async-done(((f32[16,2,4096]{2,1,0:T(2,128)}), f32[16,2,4096]{2,1,0:T(2,128)S(1)}, u32[]{:S(2)}, u32[]{:S(2)}) %all-to-all-start.2) | async-done | bytes 524320 | tf_op jit(solution)/shard_map/all_to_all | solution.py:11
  137.5 11.3 %subtract_convert_fusion = bf16[1024,4096]{1,0:T(8,128)(2,1)S(1)} fusion(f32[1024,4096]{1,0:T(8,128)} %copy-done.1, s32[4096]{0:T(1024)S(1)} %fusion.87, f32[4096]{0:T(1024)S(1)} %bitcast.120, f32[4096]{0:T(1024)S(1)} %bitcast.121, f32[1024]{0:T(1024)S(1)} %bitcast.123, f32[1024]{0:T(1024)S(1)} %bitcast.124, f32[]{:T(128)} %bitcast.116, s32[1024]{0:T(1024)S(1)} %iota_add_fusion), kind=kLoop, calls=%fused_computation | loop fusion | flops 46137344 | bytes 25227268 | tf_op jit(solution)/shard_map/convert_element_type | solution.py:136
  148.7 3.3 copy-done.5
  152.0 6.7 %multiply_convert_fusion.1 = bf16[1024,512]{1,0:T(8,128)(2,1)S(1)} fusion(bf16[1024,4096]{1,0:T(8,128)(2,1)S(1)} %subtract_convert_fusion, bf16[4096,512]{1,0:T(8,128)(2,1)} %bitcast.2, f32[]{:T(128)} %bitcast.114), kind=kOutput, calls=%fused_computation.17 | convolution fusion | flops 4296015872 | bytes 13631492 | tf_op jit(solution)/shard_map/dot_general | solution.py:137
  160.9 6.5 %all-to-all-start.3 = ((bf16[4,1024,512]{2,1,0:T(8,128)(2,1)}), bf16[4,1024,512]{2,1,0:T(8,128)(2,1)}, u32[]{:S(2)}, u32[]{:S(2)}) async-start(bf16[4,1024,512]{2,1,0:T(8,128)(2,1)} %broadcast_in_dim.53), calls=%async_computation.4 | async-start | bytes 8388608 | tf_op jit(solution)/shard_map/all_to_all | solution.py:11
  167.8 47.0 %all-to-all-done.3 = bf16[4,1024,512]{2,1,0:T(8,128)(2,1)} async-done(((bf16[4,1024,512]{2,1,0:T(8,128)(2,1)}), bf16[4,1024,512]{2,1,0:T(8,128)(2,1)}, u32[]{:S(2)}, u32[]{:S(2)}) %all-to-all-start.3) | async-done | bytes 4194336 | tf_op jit(solution)/shard_map/all_to_all | solution.py:11
  214.7 3.1 convert_reduce_fusion
  222.4 5.2 %all-to-all-start.4 = ((bf16[4,256,512]{2,1,0:T(8,128)(2,1)}), bf16[4,256,512]{2,1,0:T(8,128)(2,1)}, u32[]{:S(2)}, u32[]{:S(2)}) async-start(bf16[4,256,512]{2,1,0:T(8,128)(2,1)} %broadcast_in_dim.55), calls=%async_computation.5 | async-start | bytes 2097152 | tf_op jit(solution)/shard_map/all_to_all | solution.py:11
  228.7 12.5 %all-to-all-done.4 = bf16[4,256,512]{2,1,0:T(8,128)(2,1)} async-done(((bf16[4,256,512]{2,1,0:T(8,128)(2,1)}), bf16[4,256,512]{2,1,0:T(8,128)(2,1)}, u32[]{:S(2)}, u32[]{:S(2)}) %all-to-all-start.4) | async-done | bytes 1048608 | tf_op jit(solution)/shard_map/all_to_all | solution.py:11
  246.9 9.9 %multiply_convert_fusion = bf16[4096,512]{1,0:T(8,128)(2,1)} fusion(bf16[1024,4096]{1,0:T(8,128)(2,1)} %copy-done.5, f32[]{:T(128)} %bitcast.112, bf16[1024,512]{1,0:T(8,128)(2,1)S(1)} %copy-done.4, f32[1024]{0:T(1024)S(1)} %add_sqrt_fusion), kind=kOutput, calls=%fused_computation.6 | convolution fusion | flops 4300734464 | bytes 13635588 | tf_op jit(solution)/shard_map/dot_general | solution.py:95
  261.8 5.2 %all-to-all-start.5 = ((bf16[4,256,512]{2,1,0:T(8,128)(2,1)}), bf16[4,256,512]{2,1,0:T(8,128)(2,1)}, u32[]{:S(2)}, u32[]{:S(2)}) async-start(bf16[4,256,512]{2,1,0:T(8,128)(2,1)} %broadcast_in_dim.56), calls=%async_computation.6 | async-start | bytes 2097152 | tf_op jit(solution)/shard_map/all_to_all | solution.py:11
  267.0 13.6 %all-to-all-done.5 = bf16[4,256,512]{2,1,0:T(8,128)(2,1)} async-done(((bf16[4,256,512]{2,1,0:T(8,128)(2,1)}), bf16[4,256,512]{2,1,0:T(8,128)(2,1)}, u32[]{:S(2)}, u32[]{:S(2)}) %all-to-all-start.5) | async-done | bytes 1048608 | tf_op jit(solution)/shard_map/all_to_all | solution.py:11
  285.5 9.4 %collective-permute-done.1 = bf16[256,512]{1,0:T(8,128)(2,1)} collective-permute-done((bf16[256,512]{1,0:T(8,128)(2,1)S(1)}, bf16[256,512]{1,0:T(8,128)(2,1)}, u32[]{:S(2)}, u32[]{:S(2)}) %collective-permute-start.1) | collective-permute-done | bytes 262176 | tf_op jit(solution)/shard_map/ppermute | solution.py:51
  299.5 5.7 %all-to-all-start.6 = ((bf16[4,256,512]{2,1,0:T(8,128)(2,1)}), bf16[4,256,512]{2,1,0:T(8,128)(2,1)}, u32[]{:S(2)}, u32[]{:S(2)}) async-start(bf16[4,256,512]{2,1,0:T(8,128)(2,1)} %broadcast_in_dim.57), calls=%async_computation.7 | async-start | bytes 2097152 | tf_op jit(solution)/shard_map/all_to_all | solution.py:11
  307.4 2.3 convolution_multiply_fusion.9
  309.7 2.4 convolution_multiply_fusion.4
  312.1 6.7 %all-to-all-done.6 = bf16[4,256,512]{2,1,0:T(8,128)(2,1)} async-done(((bf16[4,256,512]{2,1,0:T(8,128)(2,1)}), bf16[4,256,512]{2,1,0:T(8,128)(2,1)}, u32[]{:S(2)}, u32[]{:S(2)}) %all-to-all-start.6) | async-done | bytes 1048608 | tf_op jit(solution)/shard_map/all_to_all | solution.py:11
  323.4 2.8 fusion.2
  326.2 6.2 %collective-permute-done.2 = bf16[256,512]{1,0:T(8,128)(2,1)S(1)} collective-permute-done((bf16[256,512]{1,0:T(8,128)(2,1)S(1)}, bf16[256,512]{1,0:T(8,128)(2,1)S(1)}, u32[]{:S(2)}, u32[]{:S(2)}) %collective-permute-start.2) | collective-permute-done | bytes 262176 | tf_op jit(solution)/shard_map/ppermute | solution.py:51
  335.6 6.0 %all-to-all-start.7 = ((bf16[4,256,512]{2,1,0:T(8,128)(2,1)}), bf16[4,256,512]{2,1,0:T(8,128)(2,1)}, u32[]{:S(2)}, u32[]{:S(2)}) async-start(bf16[4,256,512]{2,1,0:T(8,128)(2,1)} %broadcast_in_dim.58), calls=%async_computation.8 | async-start | bytes 2097152 | tf_op jit(solution)/shard_map/all_to_all | solution.py:11
  346.0 9.2 %all-to-all-done.7 = bf16[4,256,512]{2,1,0:T(8,128)(2,1)} async-done(((bf16[4,256,512]{2,1,0:T(8,128)(2,1)}), bf16[4,256,512]{2,1,0:T(8,128)(2,1)}, u32[]{:S(2)}, u32[]{:S(2)}) %all-to-all-start.7) | async-done | bytes 1048608 | tf_op jit(solution)/shard_map/all_to_all | solution.py:11
  361.2 7.6 %collective-permute-done.3 = bf16[256,512]{1,0:T(8,128)(2,1)S(1)} collective-permute-done((bf16[256,512]{1,0:T(8,128)(2,1)S(1)}, bf16[256,512]{1,0:T(8,128)(2,1)S(1)}, u32[]{:S(2)}, u32[]{:S(2)}) %collective-permute-start.3) | collective-permute-done | bytes 262176 | tf_op jit(solution)/shard_map/ppermute | solution.py:51
  373.7 5.3 %all-to-all-start.8 = ((bf16[4,256,512]{2,1,0:T(8,128)(2,1)}), bf16[4,256,512]{2,1,0:T(8,128)(2,1)S(1)}, u32[]{:S(2)}, u32[]{:S(2)}) async-start(bf16[4,256,512]{2,1,0:T(8,128)(2,1)} %broadcast_in_dim.59), calls=%async_computation.9 | async-start | bytes 2097152 | tf_op jit(solution)/shard_map/all_to_all | solution.py:11
  380.2 12.3 %all-to-all-done.8 = bf16[4,256,512]{2,1,0:T(8,128)(2,1)S(1)} async-done(((bf16[4,256,512]{2,1,0:T(8,128)(2,1)}), bf16[4,256,512]{2,1,0:T(8,128)(2,1)S(1)}, u32[]{:S(2)}, u32[]{:S(2)}) %all-to-all-start.8) | async-done | bytes 1048608 | tf_op jit(solution)/shard_map/all_to_all | solution.py:11
  397.9 43.3 %reduce-scatter.7.cloned.1.call-done = bf16[32,1024]{1,0:T(8,128)(2,1)} async-done(((bf16[512,1024]{1,0:T(8,128)(2,1)}), bf16[32,1024]{1,0:T(8,128)(2,1)}) %reduce-scatter.7.cloned.1.call-update) | async-done | bytes 65552
  (180 shorter events, 83.1 us)
Async XLA Ops:
  8.0 159.4 %copy-start = (bf16[1,1024,512]{2,1,0:T(8,128)(2,1)S(1)}, bf16[1,1024,512]{2,1,0:T(8,128)(2,1)}, u32[]{:S(2)}) copy-start(bf16[1,1024,512]{2,1,0:T(8,128)(2,1)} %param.9) | copy-start | bytes 3145732
  8.0 9.8 %copy-start.2 = (bf16[256,512]{1,0:T(8,128)(2,1)S(1)}, bf16[256,512]{1,0:T(8,128)(2,1)}, u32[]{:S(2)}) copy-start(bf16[256,512]{1,0:T(8,128)(2,1)} %param.7) | copy-start | bytes 786436
  20.8 9.5 %copy-start.4 = (bf16[1024,512]{1,0:T(8,128)(2,1)S(1)}, bf16[1024,512]{1,0:T(8,128)(2,1)}, u32[]{:S(2)}) copy-start(bf16[1024,512]{1,0:T(8,128)(2,1)} %param.6) | copy-start | bytes 3145732
  20.8 71.2 %all-to-all-start = ((bf16[16,256,512]{2,1,0:T(8,128)(2,1)}), bf16[16,256,512]{2,1,0:T(8,128)(2,1)}, u32[]{:S(2)}, u32[]{:S(2)}) async-start(bf16[16,256,512]{2,1,0:T(8,128)(2,1)} %bitcast.118), calls=%async_computation | async-start | bytes 8388608 | tf_op jit(solution)/shard_map/all_to_all | solution.py:120
  98.6 5.7 %copy-start.1 = (f32[1024,4096]{1,0:T(8,128)}, f32[1024,4096]{1,0:T(8,128)S(1)}, u32[]{:S(2)}) copy-start(f32[1024,4096]{1,0:T(8,128)S(1)} %get-tuple-element.45) | copy-start | bytes 50331652
  105.0 13.6 %all-to-all-start.1 = ((f32[4,2,1024]{2,1,0:T(2,128)}), f32[4,2,1024]{2,1,0:T(2,128)S(1)}, u32[]{:S(2)}, u32[]{:S(2)}) async-start(f32[4,2,1024]{2,1,0:T(2,128)} %broadcast_in_dim.50), calls=%async_computation.1 | async-start | bytes 65536 | tf_op jit(solution)/shard_map/all_to_all | solution.py:11
  119.5 15.4 %all-to-all-start.2 = ((f32[16,2,4096]{2,1,0:T(2,128)}), f32[16,2,4096]{2,1,0:T(2,128)S(1)}, u32[]{:S(2)}, u32[]{:S(2)}) async-start(f32[16,2,4096]{2,1,0:T(2,128)} %broadcast_in_dim.51), calls=%async_computation.2 | async-start | bytes 1048576 | tf_op jit(solution)/shard_map/all_to_all | solution.py:11
  148.7 3.3 copy-start.5
  160.9 6.5 %copy-start.3 = (bf16[1,512,512]{2,1,0:T(8,128)(2,1)S(1)}, bf16[1,512,512]{2,1,0:T(8,128)(2,1)}, u32[]{:S(2)}) copy-start(bf16[1,512,512]{2,1,0:T(8,128)(2,1)} %param.10) | copy-start | bytes 1572868
  160.9 53.8 %all-to-all-start.3 = ((bf16[4,1024,512]{2,1,0:T(8,128)(2,1)}), bf16[4,1024,512]{2,1,0:T(8,128)(2,1)}, u32[]{:S(2)}, u32[]{:S(2)}) async-start(bf16[4,1024,512]{2,1,0:T(8,128)(2,1)} %broadcast_in_dim.53), calls=%async_computation.4 | async-start | bytes 8388608 | tf_op jit(solution)/shard_map/all_to_all | solution.py:11
  167.7 51.1 %copy-start.22 = (f32[256,512]{1,0:T(8,128)}, f32[256,512]{1,0:T(8,128)S(1)}, u32[]{:S(2)}) copy-start(f32[256,512]{1,0:T(8,128)S(1)} %fusion.33) | copy-start | bytes 1572868
  217.9 2.0 copy-start.25
  222.4 18.8 %all-to-all-start.4 = ((bf16[4,256,512]{2,1,0:T(8,128)(2,1)}), bf16[4,256,512]{2,1,0:T(8,128)(2,1)}, u32[]{:S(2)}, u32[]{:S(2)}) async-start(bf16[4,256,512]{2,1,0:T(8,128)(2,1)} %broadcast_in_dim.55), calls=%async_computation.5 | async-start | bytes 2097152 | tf_op jit(solution)/shard_map/all_to_all | solution.py:11
  227.6 167.2 %reduce-scatter.5.cloned.1.call-start = ((), (), s32[]{:S(2)}) async-start(), calls=%async_computation.11 | async-start | bytes 4456448 | tf_op jit(solution)/shard_map/reduce_scatter | solution.py:140
  245.4 11.5 %collective-permute-start = (bf16[256,512]{1,0:T(8,128)(2,1)S(1)}, bf16[256,512]{1,0:T(8,128)(2,1)S(1)}, u32[]{:S(2)}, u32[]{:S(2)}) collective-permute-start(bf16[256,512]{1,0:T(8,128)(2,1)S(1)} %get-tuple-element.25), channel_id=1, source_target_pairs={{64,0},{65,1},{66,2},{67,3},{68,4},{69,5},{70,6},{71,7},{72,8},{73... | collective-permute-start | bytes 786440 | tf_op jit(solution)/shard_map/ppermute | solution.py:51
  261.8 18.8 %all-to-all-start.5 = ((bf16[4,256,512]{2,1,0:T(8,128)(2,1)}), bf16[4,256,512]{2,1,0:T(8,128)(2,1)}, u32[]{:S(2)}, u32[]{:S(2)}) async-start(bf16[4,256,512]{2,1,0:T(8,128)(2,1)} %broadcast_in_dim.56), calls=%async_computation.6 | async-start | bytes 2097152 | tf_op jit(solution)/shard_map/all_to_all | solution.py:11
  283.9 11.0 %collective-permute-start.1 = (bf16[256,512]{1,0:T(8,128)(2,1)S(1)}, bf16[256,512]{1,0:T(8,128)(2,1)}, u32[]{:S(2)}, u32[]{:S(2)}) collective-permute-start(bf16[256,512]{1,0:T(8,128)(2,1)S(1)} %get-tuple-element.23), channel_id=1, source_target_pairs={{64,0},{65,1},{66,2},{67,3},{68,4},{69,5},{70,6},{71,7},{72,8},{73... | collective-permute-start | bytes 786440 | tf_op jit(solution)/shard_map/ppermute | solution.py:51
  285.5 10.4 %copy-start.11 = (f32[256,512]{1,0:T(8,128)}, f32[256,512]{1,0:T(8,128)S(1)}, u32[]{:S(2)}) copy-start(f32[256,512]{1,0:T(8,128)S(1)} %fusion.27) | copy-start | bytes 1572868
  299.5 19.3 %all-to-all-start.6 = ((bf16[4,256,512]{2,1,0:T(8,128)(2,1)}), bf16[4,256,512]{2,1,0:T(8,128)(2,1)}, u32[]{:S(2)}, u32[]{:S(2)}) async-start(bf16[4,256,512]{2,1,0:T(8,128)(2,1)} %broadcast_in_dim.57), calls=%async_computation.7 | async-start | bytes 2097152 | tf_op jit(solution)/shard_map/all_to_all | solution.py:11
  318.8 14.3 %copy-start.23 = (f32[256,512]{1,0:T(8,128)S(1)}, f32[256,512]{1,0:T(8,128)}, u32[]{:S(2)}) copy-start(f32[256,512]{1,0:T(8,128)} %fusion.24) | copy-start | bytes 1572868
  318.8 14.3 %copy-start.26 = (bf16[1,512,512]{2,1,0:T(8,128)(2,1)S(1)}, bf16[1,512,512]{2,1,0:T(8,128)(2,1)}, u32[]{:S(2)}) copy-start(bf16[1,512,512]{2,1,0:T(8,128)(2,1)} %param.11) | copy-start | bytes 1572868
  322.1 10.3 %collective-permute-start.2 = (bf16[256,512]{1,0:T(8,128)(2,1)S(1)}, bf16[256,512]{1,0:T(8,128)(2,1)S(1)}, u32[]{:S(2)}, u32[]{:S(2)}) collective-permute-start(bf16[256,512]{1,0:T(8,128)(2,1)S(1)} %get-tuple-element.21), channel_id=1, source_target_pairs={{64,0},{65,1},{66,2},{67,3},{68,4},{69,5},{70,6},{71,7},{72,8},{73... | collective-permute-start | bytes 786440 | tf_op jit(solution)/shard_map/ppermute | solution.py:51
  335.6 19.6 %all-to-all-start.7 = ((bf16[4,256,512]{2,1,0:T(8,128)(2,1)}), bf16[4,256,512]{2,1,0:T(8,128)(2,1)}, u32[]{:S(2)}, u32[]{:S(2)}) async-start(bf16[4,256,512]{2,1,0:T(8,128)(2,1)} %broadcast_in_dim.58), calls=%async_computation.8 | async-start | bytes 2097152 | tf_op jit(solution)/shard_map/all_to_all | solution.py:11
  341.7 99.5 %reduce-scatter.7.cloned.1.call-start = ((), (), s32[]{:S(2)}) async-start(), calls=%async_computation.13 | async-start | bytes 1114112
  341.7 3.0 copy-start.16
  343.3 13.5 %copy-start.21 = (bf16[256,512]{1,0:T(8,128)(2,1)S(1)}, bf16[256,512]{1,0:T(8,128)(2,1)}, u32[]{:S(2)}) copy-start(bf16[256,512]{1,0:T(8,128)(2,1)} %copy-done.20) | copy-start | bytes 786436
  355.2 13.6 %copy-start.24 = (f32[256,512]{1,0:T(8,128)S(1)}, f32[256,512]{1,0:T(8,128)}, u32[]{:S(2)}) copy-start(f32[256,512]{1,0:T(8,128)} %fusion.21) | copy-start | bytes 1572868
  355.2 13.6 %copy-start.27 = (bf16[1,512,512]{2,1,0:T(8,128)(2,1)S(1)}, bf16[1,512,512]{2,1,0:T(8,128)(2,1)}, u32[]{:S(2)}) copy-start(bf16[1,512,512]{2,1,0:T(8,128)(2,1)} %param.11) | copy-start | bytes 1572868
  358.5 10.3 %collective-permute-start.3 = (bf16[256,512]{1,0:T(8,128)(2,1)S(1)}, bf16[256,512]{1,0:T(8,128)(2,1)S(1)}, u32[]{:S(2)}, u32[]{:S(2)}) collective-permute-start(bf16[256,512]{1,0:T(8,128)(2,1)S(1)} %get-tuple-element.19), channel_id=1, source_target_pairs={{64,0},{65,1},{66,2},{67,3},{68,4},{69,5},{70,6},{71,7},{72,8},{73... | collective-permute-start | bytes 786440 | tf_op jit(solution)/shard_map/ppermute | solution.py:51
  361.2 8.4 %copy-start.9 = (f32[512,512]{0,1:T(8,128)S(1)}, f32[512,512]{0,1:T(8,128)}, u32[]{:S(2)}) copy-start(f32[512,512]{0,1:T(8,128)} %fusion.4) | copy-start | bytes 3145732
  373.7 18.9 %all-to-all-start.8 = ((bf16[4,256,512]{2,1,0:T(8,128)(2,1)}), bf16[4,256,512]{2,1,0:T(8,128)(2,1)S(1)}, u32[]{:S(2)}, u32[]{:S(2)}) async-start(bf16[4,256,512]{2,1,0:T(8,128)(2,1)} %broadcast_in_dim.59), calls=%async_computation.9 | async-start | bytes 2097152 | tf_op jit(solution)/shard_map/all_to_all | solution.py:11
  379.0 64.7 %all-gather.2.cloned.1.call-start = ((), (), s32[]{:S(2)}) async-start(), calls=%async_computation.12 | async-start | bytes 3145728 | tf_op jit(solution)/shard_map/all_gather | solution.py:55
  (12 other events, 12.2 us)
Sparse Core Ops, SparseCore 0:
  257.0 75.8 reduce-scatter.4
  372.3 68.7 reduce-scatter.6
Sparse Core Ops, SparseCore 1:
  394.9 31.9 all-gather.1
